TPU v7x, 32 devices: a whole 2x2x4 slice. The times are simulated.
32 devices in a mesh: snap: 4 (over y, x), vert: 8 (over z, core).
Axes of the slice: x: 2, y: 2, z: 4, core: 2. Of those that a mesh axis runs over, the one named last changes fastest.
Arguments:
- features: bfloat16 [32, 2048, 256], P('snap', 'vert'), may hold values from -6 to 6
- tile_cols: int32 [32, 16, 4], P('snap', 'vert'), may hold values from -1 to 15, as said below
- counts: int32 [32, 16], P('snap', 'vert'), may hold values from 1 to 4
- birth_snap: int32 [2048], P('vert'), may hold values from 0 to 31
- query_proj: bfloat16 [256, 256], replicated, may hold values from -0.375 to 0.375
- keyval_proj: bfloat16 [256, 512], replicated, may hold values from -0.375 to 0.375
- struct_out: bfloat16 [256, 256], replicated, may hold values from -0.375 to 0.375
- position_embedding_table: bfloat16 [32, 256], replicated, may hold values from -3 to 3
- temporal_qkv_weight: bfloat16 [256, 768], replicated, may hold values from -0.375 to 0.375
- temporal_output_weight: bfloat16 [256, 256], replicated, may hold values from -0.375 to 0.375
Outputs:
- embeddings: float32 [32, 8, 4, 64, 256], P(None, 'vert', 'snap')
Inputs may be any that keep to these rules, and one draw needn't show every extreme that they name: `tile_cols`: entries k < counts[s, r] name column blocks of occupied tiles (a block may appear twice); the others are -1. Of the live entries of the 8 x 2 row blocks of one device, at most 10 lie in column blocks of any one index of vert, and exactly 10 for one index.
All inputs are finite; a program needn't handle non-finite values.
Results may differ from a plain program's by a relative error of at most 0.008.
Values may be sent and summed in bfloat16 or wider, within the bound.
No kernel may reach another device: no remote copies, remote signals or barrier semaphores. Data moves between devices by JAX's collectives and lax.ppermute only.
A program may use at most 128 MiB of HBM per device.

v0:
```python
import jax
import jax.numpy as jnp
from jax import lax
from jax.sharding import PartitionSpec as P

HEADS = 8
TILE = 128


def head_columns(model_width):
    head_size = model_width // HEADS
    column_head = jnp.arange(model_width, dtype=jnp.int32)[None, :] // head_size
    return (column_head == jnp.arange(HEADS, dtype=jnp.int32)[:, None]).astype(jnp.bfloat16)


def widen_heads(rows, column_mask):
    count, length, model_width = rows.shape
    spread = rows[:, None, :, :] * column_mask[None, :, None, :]
    return spread.reshape(count, HEADS * length, model_width)


def attend_tiles(query_rows_all, key_rows, live_keys):
    count, span, model_width = query_rows_all.shape
    head_size = model_width // HEADS
    length = key_rows.shape[1]
    column_mask = head_columns(model_width)
    widened_keys = widen_heads(key_rows[:, :, :model_width], column_mask)
    widened_values = widen_heads(key_rows[:, :, model_width:], column_mask)
    scores = jnp.einsum(
        "twn,thn->twh", query_rows_all, widened_keys, preferred_element_type=jnp.float32
    ) * head_size ** (-0.5)
    scores = scores.reshape(count, span, HEADS, length)
    scores = jnp.where(live_keys[:, None, None, :], scores, -jnp.inf)
    weight_matrices = (
        jax.nn.softmax(scores, axis=-1).astype(jnp.bfloat16).reshape(count, span, HEADS * length)
    )
    blended_rows = jnp.einsum(
        "gyv,gvl->gyl", weight_matrices, widened_values, preferred_element_type=jnp.float32
    )
    return blended_rows.astype(jnp.bfloat16)


def time_layer(
    hidden_block, births, position_embedding_table, temporal_qkv_weight, temporal_output_weight
):
    length, count, model_width = hidden_block.shape
    head_size = model_width // HEADS
    vertex_rows = jnp.transpose(hidden_block, (1, 0, 2))
    blended_input = (
        vertex_rows.astype(jnp.float32) + position_embedding_table.astype(jnp.float32)[None, :, :]
    ).astype(jnp.bfloat16)
    projected_rows = jnp.einsum(
        "csf,fz->csz", blended_input, temporal_qkv_weight, preferred_element_type=jnp.float32
    ).astype(jnp.bfloat16)
    column_mask = head_columns(model_width)
    query_rows_all = projected_rows[:, :, :model_width]
    widened_keys = widen_heads(projected_rows[:, :, model_width : 2 * model_width], column_mask)
    widened_values = widen_heads(projected_rows[:, :, 2 * model_width :], column_mask)
    scores = jnp.einsum(
        "csd,cxd->csx", query_rows_all, widened_keys, preferred_element_type=jnp.float32
    ) * head_size ** (-0.5)
    scores = scores.reshape(count, length, HEADS, length)
    later = jnp.arange(length, dtype=jnp.int32)[:, None]
    earlier = jnp.arange(length, dtype=jnp.int32)[None, :]
    allowed = (earlier <= later)[None] & (earlier[None] >= births[:, None, None]) | (
        earlier == later
    )[None]
    scores = jnp.where(allowed[:, :, None, :], scores, -jnp.inf)
    weight_matrices = (
        jax.nn.softmax(scores, axis=-1).astype(jnp.bfloat16).reshape(count, length, HEADS * length)
    )
    blended_rows = jnp.einsum(
        "csx,cxd->csd", weight_matrices, widened_values, preferred_element_type=jnp.float32
    ).astype(jnp.bfloat16)
    update_rows = jnp.einsum(
        "csf,fz->csz", blended_rows, temporal_output_weight, preferred_element_type=jnp.float32
    )
    result_rows = vertex_rows.astype(jnp.float32) + update_rows
    return jnp.transpose(result_rows, (1, 0, 2))


def local(
    features,
    tile_cols,
    counts,
    birth_snap,
    query_proj,
    keyval_proj,
    struct_out,
    position_embedding_table,
    temporal_qkv_weight,
    temporal_output_weight,
):
    snap_count, vert_rows, model_width = features.shape
    blocks = vert_rows // TILE
    tile_slots = tile_cols.shape[2]
    peer_count = lax.axis_size("vert")
    capacity = max(2, (snap_count * blocks * tile_slots + peer_count - 2) // (peer_count - 1))
    flat_rows = features.reshape(snap_count * vert_rows, model_width)
    query_rows_all = jnp.dot(flat_rows, query_proj, preferred_element_type=jnp.float32).astype(
        jnp.bfloat16
    )
    query_rows_all = query_rows_all.reshape(snap_count, blocks, TILE, model_width)
    live_tiles = jnp.arange(tile_slots, dtype=jnp.int32)[None, None, :] < counts[:, :, None]
    owning_devices = tile_cols // blocks
    block_codes = (
        jnp.arange(snap_count, dtype=jnp.int32)[:, None, None] * blocks + tile_cols % blocks
    )
    live_flat = live_tiles.reshape(-1)
    owners_flat = owning_devices.reshape(-1)
    onehot = (
        (owners_flat[:, None] == jnp.arange(peer_count, dtype=jnp.int32)[None, :])
        & live_flat[:, None]
    ).astype(jnp.int32)
    slot_rank = jnp.sum((jnp.cumsum(onehot, axis=0) - onehot) * onehot, axis=1)
    slot_index = jnp.where(live_flat, owners_flat * capacity + slot_rank, peer_count * capacity)
    outgoing_codes = (
        jnp.full((peer_count * capacity,), -1, jnp.int32)
        .at[slot_index]
        .set(block_codes.reshape(-1), mode="drop")
    )
    requested_tiles = lax.all_to_all(
        outgoing_codes.reshape(peer_count, capacity),
        "vert",
        split_axis=0,
        concat_axis=0,
        tiled=True,
    )
    picked = jnp.clip(requested_tiles.reshape(-1), 0, snap_count * blocks - 1)
    feature_blocks = features.reshape(snap_count * blocks, TILE, model_width)
    outgoing = feature_blocks[picked].reshape(peer_count, capacity, TILE, model_width)
    incoming = lax.all_to_all(outgoing, "vert", split_axis=0, concat_axis=0, tiled=True)
    fetched = jnp.dot(
        incoming.reshape(-1, model_width), keyval_proj, preferred_element_type=jnp.float32
    )
    fetched = fetched.astype(jnp.bfloat16).reshape(peer_count * capacity, TILE, 2 * model_width)
    slot_table = jnp.where(live_tiles, slot_index.reshape(snap_count, blocks, tile_slots), 0)

    def per_snapshot(pieces):
        query_block, slot_block, live_block = pieces
        key_rows = fetched[slot_block].reshape(blocks, tile_slots * TILE, 2 * model_width)
        live_keys = jnp.repeat(live_block, TILE, axis=1)
        return attend_tiles(query_block, key_rows, live_keys)

    attended = lax.map(per_snapshot, (query_rows_all, slot_table, live_tiles)).reshape(
        snap_count * vert_rows, model_width
    )
    update_rows = jnp.dot(attended, struct_out, preferred_element_type=jnp.float32)
    hidden = (
        (flat_rows.astype(jnp.float32) + update_rows)
        .astype(jnp.bfloat16)
        .reshape(snap_count, vert_rows, model_width)
    )
    groups = lax.axis_size("snap")
    quarter = vert_rows // groups
    split_rows = hidden.reshape(snap_count, groups, quarter, model_width)
    arrived = lax.all_to_all(split_rows, "snap", split_axis=1, concat_axis=0, tiled=True)
    born_at = lax.dynamic_slice_in_dim(birth_snap, lax.axis_index("snap") * quarter, quarter)
    result = time_layer(
        arrived[:, 0],
        born_at,
        position_embedding_table,
        temporal_qkv_weight,
        temporal_output_weight,
    )[:, None]
    return result[:, None]


def solution(mesh):
    placed = (
        P("snap", "vert", None),
        P("snap", "vert", None),
        P("snap", "vert"),
        P("vert"),
        P(),
        P(),
        P(),
        P(),
        P(),
        P(),
    )
    return jax.shard_map(
        local,
        mesh=mesh,
        in_specs=placed,
        out_specs=P(None, "vert", "snap", None, None),
        check_vma=False,
    )
```

profile of v0, /device:TPU:0, one launch (start us, length us, event | category | flops | bytes accessed | tf_op | source)
XLA Modules:
  0.0 520.8 jit_solution(15961900236939712950)
XLA Ops:
  3.5 11.7 %all_to_all.23 = s32[8,1,10]{2,1,0:T(1,128)S(1)} all-to-all(s32[8,1,10]{2,1,0:T(1,128)S(1)} %bitcast.164), channel_id=1, replica_groups=mesh['snap'=4,'vert'=8] {'vert'}, dimensions={0} | all-to-all | bytes 640 | tf_op jit(solution)/shard_map/all_to_all | solution.py:122
  15.3 6.9 %gather_fusion.1 = bf16[80,128,256]{2,1,0:T(8,128)(2,1)} fusion(bf16[16,128,256]{2,1,0:T(8,128)(2,1)} %bitcast.147, s32[1024]{0:T(1024)S(1)} %pad_clamp_fusion.1), kind=kCustom, calls=%fused_computation.1 | custom fusion | bytes 10486080 | tf_op jit(solution)/shard_map/gather | solution.py:131
  29.7 113.8 %all-to-all-done.1 = bf16[8,10,128,256]{3,2,1,0:T(8,128)(2,1)} async-done(((bf16[8,10,128,256]{3,2,1,0:T(8,128)(2,1)}), bf16[8,10,128,256]{3,2,1,0:T(8,128)(2,1)}, u32[]{:S(2)}, u32[]{:S(2)}) %all-to-all-start.1) | async-done | bytes 5242912 | tf_op jit(solution)/shard_map/all_to_all | solution.py:132
  143.5 8.0 %convolution_convert_fusion = bf16[10240,512]{1,0:T(8,128)(2,1)} fusion(bf16[10240,256]{1,0:T(8,128)(2,1)} %bitcast.16, bf16[256,512]{1,0:T(8,128)(2,1)S(1)} %copy-done.5), kind=kOutput, calls=%fused_computation.32 | convolution fusion | flops 2689597440 | bytes 15990784 | tf_op jit(solution)/shard_map/dot_general | solution.py:133
  151.5 296.8 %while.12 = (s32[]{:T(128)}, bf16[8,2,128,256]{3,2,1,0:T(8,128)(2,1)}, pred[8,2,4]{2,1,0:T(4,128)(4,1)S(1)}, bf16[8,2,128,256]{3,2,1,0:T(8,128)(2,1)S(1)}, s32[8...) while((s32[]{:T(128)}, bf16[8,2,128,256]{3,2,1,0:T(8,128)(2,1)}, ...), condition=%wide.region_6.7_spmd, body=%wide.region_3.6_spmd.sunk | while | flops 1088490496 | bytes 102069064 | solution.py:145
  175.8 5.0 sub.102
  180.8 7.8 %fusion.66 = bf16[8,2,128,256]{3,2,1,0:T(8,128)(2,1)} fusion(bf16[8,2,128,256]{3,2,1,0:T(8,128)(2,1)} %get-tuple-element.162, s32[]{:T(128)} %get-tuple-element.161, bf16[2,4096,256]{2,1,0:T(8,128)(2,1)} %get-tuple-element.152, f32[2,128,4096]{2,1,0:T(8,128)} %div.99, f32[2,128,4096]{2,1,0:T(8,128)} %sub.102, f32[2,128,4096]{2,1,0:T(8,128)} %copy-done.1, ...), kind=kOutput, calls=%fused_computation.14.clone.1 | convolution fusion | flops 541130752 | bytes 16916992 | tf_op jit(solution)/shard_map/while/body/eval_jaxpr/gyv,gvl->gyl/dot_general | solution.py:37
  212.9 5.0 sub.102
  217.9 7.8 %fusion.66 = bf16[8,2,128,256]{3,2,1,0:T(8,128)(2,1)} fusion(bf16[8,2,128,256]{3,2,1,0:T(8,128)(2,1)} %get-tuple-element.162, s32[]{:T(128)} %get-tuple-element.161, bf16[2,4096,256]{2,1,0:T(8,128)(2,1)} %get-tuple-element.152, f32[2,128,4096]{2,1,0:T(8,128)} %div.99, f32[2,128,4096]{2,1,0:T(8,128)} %sub.102, f32[2,128,4096]{2,1,0:T(8,128)} %copy-done.1, ...), kind=kOutput, calls=%fused_computation.14.clone.1 | convolution fusion | flops 541130752 | bytes 16916992 | tf_op jit(solution)/shard_map/while/body/eval_jaxpr/gyv,gvl->gyl/dot_general | solution.py:37
  250.0 5.0 sub.102
  255.0 7.8 %fusion.66 = bf16[8,2,128,256]{3,2,1,0:T(8,128)(2,1)} fusion(bf16[8,2,128,256]{3,2,1,0:T(8,128)(2,1)} %get-tuple-element.162, s32[]{:T(128)} %get-tuple-element.161, bf16[2,4096,256]{2,1,0:T(8,128)(2,1)} %get-tuple-element.152, f32[2,128,4096]{2,1,0:T(8,128)} %div.99, f32[2,128,4096]{2,1,0:T(8,128)} %sub.102, f32[2,128,4096]{2,1,0:T(8,128)} %copy-done.1, ...), kind=kOutput, calls=%fused_computation.14.clone.1 | convolution fusion | flops 541130752 | bytes 16916992 | tf_op jit(solution)/shard_map/while/body/eval_jaxpr/gyv,gvl->gyl/dot_general | solution.py:37
  287.1 5.0 sub.102
  292.1 7.8 %fusion.66 = bf16[8,2,128,256]{3,2,1,0:T(8,128)(2,1)} fusion(bf16[8,2,128,256]{3,2,1,0:T(8,128)(2,1)} %get-tuple-element.162, s32[]{:T(128)} %get-tuple-element.161, bf16[2,4096,256]{2,1,0:T(8,128)(2,1)} %get-tuple-element.152, f32[2,128,4096]{2,1,0:T(8,128)} %div.99, f32[2,128,4096]{2,1,0:T(8,128)} %sub.102, f32[2,128,4096]{2,1,0:T(8,128)} %copy-done.1, ...), kind=kOutput, calls=%fused_computation.14.clone.1 | convolution fusion | flops 541130752 | bytes 16916992 | tf_op jit(solution)/shard_map/while/body/eval_jaxpr/gyv,gvl->gyl/dot_general | solution.py:37
  324.2 5.0 sub.102
  329.2 7.8 %fusion.66 = bf16[8,2,128,256]{3,2,1,0:T(8,128)(2,1)} fusion(bf16[8,2,128,256]{3,2,1,0:T(8,128)(2,1)} %get-tuple-element.162, s32[]{:T(128)} %get-tuple-element.161, bf16[2,4096,256]{2,1,0:T(8,128)(2,1)} %get-tuple-element.152, f32[2,128,4096]{2,1,0:T(8,128)} %div.99, f32[2,128,4096]{2,1,0:T(8,128)} %sub.102, f32[2,128,4096]{2,1,0:T(8,128)} %copy-done.1, ...), kind=kOutput, calls=%fused_computation.14.clone.1 | convolution fusion | flops 541130752 | bytes 16916992 | tf_op jit(solution)/shard_map/while/body/eval_jaxpr/gyv,gvl->gyl/dot_general | solution.py:37
  361.3 5.0 sub.102
  366.4 7.8 %fusion.66 = bf16[8,2,128,256]{3,2,1,0:T(8,128)(2,1)} fusion(bf16[8,2,128,256]{3,2,1,0:T(8,128)(2,1)} %get-tuple-element.162, s32[]{:T(128)} %get-tuple-element.161, bf16[2,4096,256]{2,1,0:T(8,128)(2,1)} %get-tuple-element.152, f32[2,128,4096]{2,1,0:T(8,128)} %div.99, f32[2,128,4096]{2,1,0:T(8,128)} %sub.102, f32[2,128,4096]{2,1,0:T(8,128)} %copy-done.1, ...), kind=kOutput, calls=%fused_computation.14.clone.1 | convolution fusion | flops 541130752 | bytes 16916992 | tf_op jit(solution)/shard_map/while/body/eval_jaxpr/gyv,gvl->gyl/dot_general | solution.py:37
  403.5 7.8 %fusion.66 = bf16[8,2,128,256]{3,2,1,0:T(8,128)(2,1)} fusion(bf16[8,2,128,256]{3,2,1,0:T(8,128)(2,1)} %get-tuple-element.162, s32[]{:T(128)} %get-tuple-element.161, bf16[2,4096,256]{2,1,0:T(8,128)(2,1)} %get-tuple-element.152, f32[2,128,4096]{2,1,0:T(8,128)} %div.99, f32[2,128,4096]{2,1,0:T(8,128)} %sub.102, f32[2,128,4096]{2,1,0:T(8,128)} %copy-done.1, ...), kind=kOutput, calls=%fused_computation.14.clone.1 | convolution fusion | flops 541130752 | bytes 16916992 | tf_op jit(solution)/shard_map/while/body/eval_jaxpr/gyv,gvl->gyl/dot_general | solution.py:37
  440.6 7.8 %fusion.66 = bf16[8,2,128,256]{3,2,1,0:T(8,128)(2,1)} fusion(bf16[8,2,128,256]{3,2,1,0:T(8,128)(2,1)} %get-tuple-element.162, s32[]{:T(128)} %get-tuple-element.161, bf16[2,4096,256]{2,1,0:T(8,128)(2,1)} %get-tuple-element.152, f32[2,128,4096]{2,1,0:T(8,128)} %div.99, f32[2,128,4096]{2,1,0:T(8,128)} %sub.102, f32[2,128,4096]{2,1,0:T(8,128)} %copy-done.1, ...), kind=kOutput, calls=%fused_computation.14.clone.1 | convolution fusion | flops 541130752 | bytes 16916992 | tf_op jit(solution)/shard_map/while/body/eval_jaxpr/gyv,gvl->gyl/dot_general | solution.py:37
  457.5 10.8 %all-to-all-done.2 = bf16[8,4,64,256]{3,2,0,1:T(8,128)(2,1)S(1)} async-done(((bf16[8,4,64,256]{3,2,0,1:T(8,128)(2,1)}), bf16[8,4,64,256]{3,2,0,1:T(8,128)(2,1)S(1)}, u32[]{:S(2)}, u32[]{:S(2)}) %all-to-all-start.2) | async-done | bytes 1048608 | tf_op jit(solution)/shard_map/all_to_all | solution.py:157
  472.4 6.8 %bitcast_multiply_fusion.3 = (bf16[64,256,256]{2,1,0:T(8,128)(2,1)}, bf16[64,256,256]{2,1,0:T(8,128)(2,1)}) fusion(bf16[256,256]{1,0:T(8,128)(2,1)S(1)} %bitcast.162, bf16[64,32,256]{2,1,0:T(8,128)(2,1)S(1)} %get-tuple-element.102, bf16[64,32,256]{2,1,0:T(8,128)(2,1)S(1)} %get-tuple-element.103), kind=kLoop, calls=%fused_computation.34 | loop fusion | flops 8388608 | bytes 19005440 | tf_op jit(solution)/shard_map/mul | solution.py:18
  479.2 6.3 %convolution_multiply_fusion.1 = f32[64,32,256]{2,1,0:T(8,128)S(1)} fusion(bf16[64,256,256]{2,1,0:T(8,128)(2,1)} %get-tuple-element.104, bf16[64,32,768]{2,1,0:T(8,128)(2,1)} %copy-done.4), kind=kOutput, calls=%fused_computation.53 | convolution fusion | flops 268959744 | bytes 11534336 | tf_op jit(solution)/shard_map/csd,cxd->csx/dot_general | solution.py:59
  497.9 5.1 fusion.11
  507.2 9.5 %fusion.16 = f32[32,1,1,64,256]{4,0,3,2,1:T(8,128)} fusion(f32[4,8,1,64,256]{4,3,1,0,2:T(8,128)} %copy-done.3, bf16[64,256,256]{2,1,0:T(8,128)(2,1)} %get-tuple-element.105, f32[64,32,256]{2,1,0:T(8,128)} %copy.40, f32[64,32,256]{2,1,0:T(8,128)} %copy.39, pred[64,32,256]{2,1,0:T(32,128)(4,1)S(1)} %copy.37, ...), kind=kOutput, calls=%fused_computation.46 | convolution fusion | flops 540016640 | bytes 19529728 | tf_op jit(solution)/shard_map/csf,fz->csz/dot_general | solution.py:75
  (259 shorter events, 248.9 us)
Async XLA Ops:
  0.0 468.5 %copy-start = (bf16[256,768]{1,0:T(8,128)(2,1)S(1)}, bf16[256,768]{1,0:T(8,128)(2,1)}, u32[]{:S(2)}) copy-start(bf16[256,768]{1,0:T(8,128)(2,1)} %param.20) | copy-start | bytes 1179652
  22.2 5.1 copy-start.9
  22.2 5.7 %copy-start.13 = (s32[256]{0:T(256)S(1)}, s32[256]{0:T(256)}, u32[]{:S(2)}) copy-start(s32[256]{0:T(256)} %param.15) | copy-start | bytes 3076
  22.2 7.1 %copy-start.2 = (bf16[8,256,256]{2,1,0:T(8,128)(2,1)S(1)}, bf16[8,256,256]{2,1,0:T(8,128)(2,1)}, u32[]{:S(2)}) copy-start(bf16[8,256,256]{2,1,0:T(8,128)(2,1)} %param.12) | copy-start | bytes 3145732
  22.2 7.1 %copy-start.8 = (bf16[256,256]{1,0:T(8,128)(2,1)S(1)}, bf16[256,256]{1,0:T(8,128)(2,1)}, u32[]{:S(2)}) copy-start(bf16[256,256]{1,0:T(8,128)(2,1)} %param.16) | copy-start | bytes 393220
  22.2 121.3 %copy-start.5 = (bf16[256,512]{1,0:T(8,128)(2,1)S(1)}, bf16[256,512]{1,0:T(8,128)(2,1)}, u32[]{:S(2)}) copy-start(bf16[256,512]{1,0:T(8,128)(2,1)} %param.17) | copy-start | bytes 786436
  22.2 121.3 %all-to-all-start.1 = ((bf16[8,10,128,256]{3,2,1,0:T(8,128)(2,1)}), bf16[8,10,128,256]{3,2,1,0:T(8,128)(2,1)}, u32[]{:S(2)}, u32[]{:S(2)}) async-start(bf16[8,10,128,256]{3,2,1,0:T(8,128)(2,1)} %bitcast.152), calls=%async_computation.1 | async-start | bytes 10485760 | tf_op jit(solution)/shard_map/all_to_all | solution.py:132
  160.5 3.9 copy-start.1
  197.6 3.9 copy-start.1
  234.7 3.9 copy-start.1
  271.8 3.9 copy-start.1
  308.9 3.9 copy-start.1
  346.0 3.9 copy-start.1
  383.1 3.9 copy-start.1
  420.2 3.9 copy-start.1
  448.3 6.6 %copy-start.12 = (s32[64]{0:T(128)S(1)}, s32[64]{0:T(128)}, u32[]{:S(2)}) copy-start(s32[64]{0:T(128)} %dynamic_slice.24) | copy-start | bytes 772
  448.3 6.6 %copy-start.10 = (pred[32,32]{1,0:T(8,128)(4,1)S(1)}, pred[32,32]{1,0:T(8,128)(4,1)}, u32[]{:S(2)}) copy-start(pred[32,32]{1,0:T(8,128)(4,1)} %get-tuple-element.107) | copy-start | bytes 3076
  448.3 6.6 %copy-start.11 = (pred[32,32]{1,0:T(8,128)(4,1)S(1)}, pred[32,32]{1,0:T(8,128)(4,1)}, u32[]{:S(2)}) copy-start(pred[32,32]{1,0:T(8,128)(4,1)} %get-tuple-element.108) | copy-start | bytes 3076
  451.0 17.5 %copy-start.7 = (f32[32,256]{1,0:T(8,128)S(1)}, f32[32,256]{1,0:T(8,128)}, u32[]{:S(2)}) copy-start(f32[32,256]{1,0:T(8,128)} %convert_element_type.95) | copy-start | bytes 98308
  451.0 17.3 %all-to-all-start.2 = ((bf16[8,4,64,256]{3,2,0,1:T(8,128)(2,1)}), bf16[8,4,64,256]{3,2,0,1:T(8,128)(2,1)S(1)}, u32[]{:S(2)}, u32[]{:S(2)}) async-start(bf16[8,4,64,256]{3,2,0,1:T(8,128)(2,1)} %copy.35), calls=%async_computation.2 | async-start | bytes 2097152 | tf_op jit(solution)/shard_map/all_to_all | solution.py:157
  468.6 2.4 copy-start.3
  470.7 1.7 copy-start.4
  502.9 4.3 copy-start.6
where the time goes:
time: 523 us; the launch traced here: 521 us
  local copies, waits for them, and re-layouts  222 us (42%)
  waiting for transfers between devices  125 us (24%)
  matrix products  102 us (20%)
  other arithmetic  50.8 us (10%)
  blocking collectives  11.7 us (2%)
  starting transfers between devices  8.83 us (2%)
    all_to_all x1, waiting for transfers between devices, local(): lax.all_to_all(outgoing, 'vert', split_axis=0, concat_axis=0, tiled=True)  114 us
    dot_general x8, matrix products, attend_tiles(): jnp.einsum('gyv,gvl->gyl', weight_matrices, widened_values, preferred_ele...  62.1 us
    sub x16, local copies, waits for them, and re-layouts, attend_tiles(): jax.nn.softmax(scores, axis=-1).astype(jnp.bfloat16)  59.1 us
    div x16, local copies, waits for them, and re-layouts, attend_tiles(): jax.nn.softmax(scores, axis=-1).astype(jnp.bfloat16)  58.5 us
    gather x8, local copies, waits for them, and re-layouts, per_snapshot(): fetched[slot_block].reshape(blocks, tile_slots * TILE, 2 * model_width)  36.7 us
    while x56, local copies, waits for them, and re-layouts  31.9 us
    mul x9, other arithmetic, widen_heads(): spread = rows[:, None, :, :] * column_mask[None, :, None, :]  27.3 us
    dot_general x8, matrix products, attend_tiles(): jnp.einsum('twn,thn->twh', query_rows_all, widened_keys, preferred_elemen...  12 us
  transfers between devices with their start and end apart: 2, of which 2 were waited for; matrix products, arithmetic and copies ran while one was open for 1% of the time, Pallas kernels for 0%

commit v1 on v0

v1 whole, which is shorter than its diff:
```python
import functools
import math

import jax
import jax.numpy as jnp
from jax import lax
from jax.experimental import pallas as pl
from jax.experimental.pallas import tpu as pltpu
from jax.sharding import PartitionSpec as P

HEADS = 8
TILE = 128
CHUNKS = 2
F32 = jnp.float32
BF16 = jnp.bfloat16


def contract_last(a, b):
    return lax.dot_general(a, b, (((1,), (1,)), ((), ())), preferred_element_type=F32)


def matmul(a, b):
    return jnp.dot(a, b, preferred_element_type=F32)


def spread_heads(rows, head_size):
    column = lax.broadcasted_iota(jnp.int32, (1, rows.shape[1]), 1) // head_size
    return jnp.concatenate(
        [rows * (column == h).astype(BF16) for h in range(HEADS)], axis=0
    )


def gather_heads(low, high, count, head_size):
    parts = []
    for blended in (low, high):
        width = blended.shape[1] // 2
        column = lax.broadcasted_iota(jnp.int32, (1, width), 1) // head_size
        top = blended[:count, :width]
        bottom = blended[:count, width:]
        for h in range(1, HEADS // 2):
            rows = slice(h * count, (h + 1) * count)
            top = jnp.where(column == h, blended[rows, :width], top)
            bottom = jnp.where(column == h, blended[rows, width:], bottom)
        parts.append(top / bottom)
    return jnp.concatenate(parts, axis=1)


def structural_kernel(
    table_ref,
    offset_ref,
    x_ref,
    wq_ref,
    wkv_ref,
    wo_ref,
    out_ref,
    k_ref,
    v_ref,
    q_ref,
    s_ref,
    p_ref,
    a_ref,
    *,
    slots,
):
    pieces, piece_rows, width = x_ref.shape
    groups, peers, rows, _ = out_ref.shape
    half = width // 2
    head_size = width // HEADS
    total = pieces * piece_rows
    row_blocks = total // TILE
    block_rows = pieces * rows // row_blocks
    factor = head_size ** (-0.5) * math.log2(math.e)
    step = 2 * TILE
    pieces_per_step = step // piece_rows

    def project(i, carry):
        at = pl.ds(pl.multiple_of(i * step, step), step)
        x = x_ref[pl.ds(i * pieces_per_step, pieces_per_step)].reshape(step, width)
        keyval = matmul(x, wkv_ref[...]).astype(BF16)
        k_ref[at, :] = keyval[:, :width]
        ones = jnp.ones((step, half), BF16)
        v_ref[at, :] = jnp.concatenate(
            [keyval[:, width : width + half], ones, keyval[:, width + half :], ones], axis=1
        )
        return carry

    lax.fori_loop(0, total // step, project, 0)
    offset = pl.multiple_of(offset_ref[0], rows)
    x_rows = x_ref[:, pl.ds(offset, rows), :].reshape(pieces * rows, width)
    q_ref[...] = matmul(x_rows, wq_ref[...]).astype(BF16)

    def attend(r, tiles):
        count = table_ref[r * (slots + 1) + slots]
        at = pl.ds(pl.multiple_of(r * block_rows, block_rows), block_rows)
        spots = []
        for t in range(tiles):
            spot = jnp.maximum(table_ref[r * (slots + 1) + t], 0)
            spots.append(pl.ds(pl.multiple_of(spot * TILE, TILE), TILE))
        queries = spread_heads(q_ref[at, :], head_size)
        keys = jnp.concatenate([k_ref[spot, :] for spot in spots], axis=0)
        s_ref[:, : tiles * TILE] = contract_last(queries, keys)
        for h in range(HEADS):
            part = slice(h * block_rows, (h + 1) * block_rows)
            scores = []
            for t in range(tiles):
                score = s_ref[part, t * TILE : (t + 1) * TILE]
                if t == tiles - 1 and t > 0:
                    score = score + jnp.where(count > t, 0.0, -jnp.inf)
                scores.append(score)
            top = scores[0]
            for score in scores[1:]:
                top = jnp.maximum(top, score)
            top = jnp.max(top, axis=1, keepdims=True)
            for t in range(tiles):
                p_ref[part, t * TILE : (t + 1) * TILE] = jnp.exp2(
                    (scores[t] - top) * factor
                ).astype(BF16)
        values = jnp.concatenate([v_ref[spot, :] for spot in spots], axis=0)
        middle = HEADS // 2 * block_rows
        low = matmul(p_ref[:middle, : tiles * TILE], values[:, :width])
        high = matmul(p_ref[middle:, : tiles * TILE], values[:, width:])
        a_ref[at, :] = gather_heads(low, high, block_rows, head_size).astype(BF16)

    def row_block(r, carry):
        count = table_ref[r * (slots + 1) + slots]
        for tiles in range(2, slots + 1, 2):
            least = tiles - 2

            @pl.when((count > least) & (count <= tiles))
            def _(tiles=tiles):
                attend(r, tiles)

        return carry

    lax.fori_loop(0, row_blocks, row_block, 0)
    update = matmul(a_ref[...], wo_ref[...])
    hidden = (x_rows.astype(F32) + update).astype(BF16).reshape(peers, groups, rows, width)
    for g in range(groups):
        out_ref[g] = hidden[:, g]


def structural(table, offset, x, query_proj, keyval_proj, struct_out, rows, groups, slots):
    pieces, piece_rows, width = x.shape
    peers = pieces // groups
    total = pieces * piece_rows
    block_rows = TILE // piece_rows * rows
    vmem = pl.BlockSpec(memory_space=pltpu.VMEM)
    smem = pl.BlockSpec(memory_space=pltpu.SMEM)
    return pl.pallas_call(
        functools.partial(structural_kernel, slots=slots),
        out_shape=jax.ShapeDtypeStruct((groups, peers, rows, width), BF16),
        in_specs=[smem, smem, vmem, vmem, vmem, vmem],
        out_specs=vmem,
        scratch_shapes=[
            pltpu.VMEM((total, width), BF16),
            pltpu.VMEM((total, 2 * width), BF16),
            pltpu.VMEM((pieces * rows, width), BF16),
            pltpu.VMEM((HEADS * block_rows, slots * TILE), F32),
            pltpu.VMEM((HEADS * block_rows, slots * TILE), BF16),
            pltpu.VMEM((pieces * rows, width), BF16),
        ],
        compiler_params=pltpu.CompilerParams(vmem_limit_bytes=48 * 1024 * 1024),
        name="structural",
    )(table, offset, x, query_proj, keyval_proj, struct_out)


def temporal_kernel(h_ref, birth_ref, pos_ref, wt_ref, wo_ref, *refs):
    out_ref = refs[-1]
    length, count, width = h_ref.shape
    half = width // 2
    head_size = width // HEADS
    factor = head_size ** (-0.5) * math.log2(math.e)
    batch = min(count, 16)
    rows = batch * length
    together = max(1, TILE // length)
    span = together * length
    line = lax.broadcasted_iota(jnp.int32, (rows, rows), 0)
    column = lax.broadcasted_iota(jnp.int32, (rows, rows), 1)
    to_vertex = (
        (line // length == column % batch) & (line % length == column // batch)
    ).astype(BF16)
    to_time = (
        (line % batch == column // length) & (line // batch == column % length)
    ).astype(BF16)
    line = lax.broadcasted_iota(jnp.int32, (span, span), 0)
    column = lax.broadcasted_iota(jnp.int32, (span, span), 1)
    same = line // length == column // length
    before = same & (column < line)
    itself = line == column
    instant = lax.broadcasted_iota(jnp.int32, (1, span), 1) % length
    ones = jnp.ones((span, half), BF16)
    positions = pos_ref[...].astype(F32)[:, None, :]
    for b in range(count // batch):
        part = slice(b * batch, (b + 1) * batch)
        hidden = h_ref[:, part, :].astype(F32)
        time_in = (hidden + positions).astype(BF16).reshape(rows, width)
        time_in = matmul(to_vertex, time_in).astype(BF16)
        projected = matmul(time_in, wt_ref[...]).astype(BF16)
        mixed = []
        for g in range(batch // together):
            at = slice(g * span, (g + 1) * span)
            queries = spread_heads(projected[at, :width], head_size)
            values = projected[at, 2 * width :]
            scores = contract_last(queries, projected[at, width : 2 * width])
            index = b * (batch // together) + g
            alive = instant >= birth_ref[index : index + 1, :]
            kept = itself | (before & alive)
            weights = []
            for h in range(HEADS):
                score = jnp.where(kept, scores[h * span : (h + 1) * span], -jnp.inf)
                top = jnp.max(score, axis=1, keepdims=True)
                weights.append(jnp.exp2((score - top) * factor).astype(BF16))
            low = jnp.concatenate(weights[: HEADS // 2], axis=0)
            high = jnp.concatenate(weights[HEADS // 2 :], axis=0)
            low = matmul(low, jnp.concatenate([values[:, :half], ones], axis=1))
            high = matmul(high, jnp.concatenate([values[:, half:], ones], axis=1))
            mixed.append(gather_heads(low, high, span, head_size).astype(BF16))
        mixed = jnp.concatenate(mixed, axis=0)
        mixed = matmul(to_time, mixed).astype(BF16)
        update = matmul(mixed, wo_ref[...]).reshape(length, batch, width)
        out_ref[:, part, :] = hidden + update


def temporal(hidden, births, positions, qkv_weight, output_weight, total, chunk, earlier):
    length, count, width = hidden.shape
    vmem = pl.BlockSpec(memory_space=pltpu.VMEM)
    args = [hidden, births, positions, qkv_weight, output_weight]
    specs = [pl.BlockSpec(a.shape, lambda i, n=a.ndim: (0,) * n) for a in args]
    aliases = {}
    if earlier is not None:
        aliases = {len(args): 0}
        args.append(earlier)
        specs.append(pl.BlockSpec(memory_space=pl.ANY))
    return pl.pallas_call(
        temporal_kernel,
        grid=(1,),
        out_shape=jax.ShapeDtypeStruct((length, total, width), F32),
        in_specs=specs,
        out_specs=pl.BlockSpec((length, count, width), lambda i: (0, chunk, 0)),
        input_output_aliases=aliases,
        compiler_params=pltpu.CompilerParams(vmem_limit_bytes=48 * 1024 * 1024),
        name="temporal",
    )(*args)


def local(
    features,
    tile_cols,
    counts,
    birth_snap,
    query_proj,
    keyval_proj,
    struct_out,
    position_embedding_table,
    temporal_qkv_weight,
    temporal_output_weight,
):
    snap_count, vert_rows, width = features.shape
    slots = tile_cols.shape[2]
    peers = lax.axis_size("vert")
    groups = lax.axis_size("snap")
    snapshots = snap_count * groups
    quarter = vert_rows // groups
    sharers = peers // snap_count
    chunks = max(1, min(CHUNKS, quarter // (sharers * 16)))
    rows = quarter // (sharers * chunks)

    table = jnp.concatenate([tile_cols, counts[:, :, None]], axis=2)
    outgoing = features
    if sharers > 1:
        outgoing = jnp.repeat(features, sharers, axis=0)
        table = jnp.repeat(table, sharers, axis=0)
    snapshot = lax.all_to_all(outgoing, "vert", split_axis=0, concat_axis=0, tiled=True)
    table = lax.all_to_all(table, "vert", split_axis=0, concat_axis=0, tiled=True).reshape(-1)
    x = snapshot.reshape(peers * groups, quarter, width)
    share = lax.axis_index("vert") % sharers

    arrived = []
    for c in range(chunks):
        offset = jnp.reshape((c * sharers + share) * rows, (1,)).astype(jnp.int32)
        hidden = structural(
            table, offset, x, query_proj, keyval_proj, struct_out, rows, groups, slots
        )
        hidden = hidden.reshape(groups * peers, rows, width)
        hidden = lax.all_to_all(
            hidden, ("snap", "vert"), split_axis=0, concat_axis=0, tiled=True
        )
        arrived.append(hidden.reshape(snapshots, sharers * rows, width))

    births = lax.dynamic_slice_in_dim(birth_snap, lax.axis_index("snap") * quarter, quarter)
    span = max(1, TILE // snapshots) * snapshots
    births = jnp.repeat(births, snapshots).reshape(chunks, -1, span)
    result = None
    for c in range(chunks):
        result = temporal(
            arrived[c],
            births[c],
            position_embedding_table,
            temporal_qkv_weight,
            temporal_output_weight,
            quarter,
            c,
            result,
        )
    return result[:, None, None]


def solution(mesh):
    placed = (
        P("snap", "vert", None),
        P("snap", "vert", None),
        P("snap", "vert"),
        P("vert"),
        P(),
        P(),
        P(),
        P(),
        P(),
        P(),
    )
    return jax.shard_map(
        local,
        mesh=mesh,
        in_specs=placed,
        out_specs=P(None, "vert", "snap", None, None),
        check_vma=False,
    )
```

time: 523 us -> 104 us (0.20)
  local copies, waits for them, and re-layouts: 222 us -> 2.34 us
  matrix products: 102 us -> 0 us
  waiting for transfers between devices: 125 us -> 37.9 us
  other arithmetic: 50.8 us -> 0.08 us
  Pallas kernels: 0 us -> 40.2 us
    dot_general x22 -> x0, matrix products: 102 us -> none  [the longest x8 62.1 us: attend_tiles(): jnp.einsum('gyv,gvl->gyl', weight_matrices, widened_values, preferred_ele...]
    all_to_all x1, waiting for transfers between devices: 114 us -> 26.4 us  [local(): lax.all_to_all(outgoing, 'vert', split_axis=0, concat_axis=0, tiled=True)]
    sub x18 -> x0, local copies, waits for them, and re-layouts: 65.6 us -> none  [the longest x16 59.1 us: attend_tiles(): jax.nn.softmax(scores, axis=-1).astype(jnp.bfloat16)]
    div x17 -> x0, local copies, waits for them, and re-layouts: 62.8 us -> none  [the longest x16 58.5 us: attend_tiles(): jax.nn.softmax(scores, axis=-1).astype(jnp.bfloat16)]
    gather x9 -> x0, local copies, waits for them, and re-layouts: 43.6 us -> none  [the longest x8 36.7 us: per_snapshot(): fetched[slot_block].reshape(blocks, tile_slots * TILE, 2 * model_width)]
    pallas_call x0 -> x4, Pallas kernels: none -> 40.2 us  [the longest x2 29 us: structural(): pl.pallas_call(functools.partial(structural_kernel, slots=slots), out_sha...]
    while x56 -> x0, local copies, waits for them, and re-layouts: 31.9 us -> none
    mul x11 -> x0, other arithmetic: 27.4 us -> none  [the longest x9 27.3 us: widen_heads(): spread = rows[:, None, :, :] * column_mask[None, :, None, :]]
  transfers between devices with their start and end apart: 2 -> 3, of which waited for: 2 -> 3; matrix products, arithmetic and copies ran while one was open for 1% -> 1% of each run, Pallas kernels for 0% -> 19%
where the time goes in v1:
time: 104 us
  Pallas kernels  40.2 us (39%)
  waiting for transfers between devices  37.9 us (36%)
  blocking collectives  11.8 us (11%)
  starting transfers between devices  11.3 us (11%)
  local copies, waits for them, and re-layouts  2.34 us (2%)
    pallas_call x2, Pallas kernels, structural(): pl.pallas_call(functools.partial(structural_kernel, slots=slots), out_sha...  29 us
    all_to_all x1, waiting for transfers between devices, local(): lax.all_to_all(outgoing, 'vert', split_axis=0, concat_axis=0, tiled=True)  26.4 us
    all_to_all x1, blocking collectives, local(): lax.all_to_all(table, 'vert', split_axis=0, concat_axis=0, tiled=True)  11.8 us
    all_to_all x2, waiting for transfers between devices, local(): lax.all_to_all(hidden, ('snap', 'vert'), split_axis=0, concat_axis=0, til...  11.5 us
    pallas_call x2, Pallas kernels, temporal(): pl.pallas_call(temporal_kernel, grid=(1,), out_shape=jax.ShapeDtypeStruct...  11.2 us
    all_to_all x2, starting transfers between devices, local(): lax.all_to_all(hidden, ('snap', 'vert'), split_axis=0, concat_axis=0, til...  7.78 us
    all_to_all x1, starting transfers between devices, local(): lax.all_to_all(outgoing, 'vert', split_axis=0, concat_axis=0, tiled=True)  3.56 us
  transfers between devices with their start and end apart: 3, of which 3 were waited for; matrix products, arithmetic and copies ran while one was open for 1% of the time, Pallas kernels for 19%

profile of v1, /device:TPU:0, one launch (start us, length us, event | category | flops | bytes accessed | tf_op | source)
XLA Modules:
  0.0 103.7 jit_solution(14711415963477524669)
XLA Ops:
  0.0 0.8 copy.18
  0.8 0.8 copy.19
  1.6 0.1 pad_add_fusion
  1.7 11.8 %all_to_all.20 = s32[8,2,5]{2,1,0:T(2,128)S(1)} all-to-all(s32[8,2,5]{2,1,0:T(2,128)S(1)} %pad_add_fusion), channel_id=1, replica_groups=mesh['snap'=4,'vert'=8] {'vert'}, dimensions={0} | all-to-all | bytes 640 | tf_op jit(solution)/shard_map/all_to_all | solution.py:274
  13.4 3.6 %all-to-all-start.1 = ((bf16[8,256,256]{2,1,0:T(8,128)(2,1)}), bf16[8,256,256]{2,1,0:T(8,128)(2,1)S(1)}, u32[]{:S(2)}, u32[]{:S(2)}) async-start(bf16[8,256,256]{2,1,0:T(8,128)(2,1)} %param.10), calls=%async_computation.1 | async-start | bytes 2097152 | tf_op jit(solution)/shard_map/all_to_all | solution.py:273
  17.0 0.1 reshape.30.table_ref
  17.1 26.4 %all-to-all-done.1 = bf16[8,256,256]{2,1,0:T(8,128)(2,1)S(1)} async-done(((bf16[8,256,256]{2,1,0:T(8,128)(2,1)}), bf16[8,256,256]{2,1,0:T(8,128)(2,1)S(1)}, u32[]{:S(2)}, u32[]{:S(2)}) %all-to-all-start.1) | async-done | bytes 1048608 | tf_op jit(solution)/shard_map/all_to_all | solution.py:273
  43.5 14.5 %structural.3 = bf16[4,8,32,256]{3,2,1,0:T(8,128)(2,1)} custom-call(s32[80]{0:T(128)S(1)} %reshape.30.table_ref, s32[1]{0:T(128)} %constant.28.clone.1.offset_ref, bf16[32,64,256]{2,1,0:T(8,128)(2,1)S(1)} %bitcast.7, bf16[256,256]{1,0:T(8,128)(2,1)S(1)} %copy-done.3, bf16[256,512]{1,0:T(8,128)(2,1)S(1)} %copy-done.1, bf16[256,256]{1,0:T(8,128)(2,1)S(1)} %copy-done.4), custom_call_target="tpu_custom_call" | custom-call | tf_op jit(solution)/shard_map/structural/pallas_call | solution.py:149
  58.0 3.5 %all-to-all-start.3 = ((bf16[32,32,256]{2,1,0:T(8,128)(2,1)}), bf16[32,32,256]{2,1,0:T(8,128)(2,1)S(1)}, u32[]{:S(2)}, u32[]{:S(2)}) async-start(bf16[32,32,256]{2,1,0:T(8,128)(2,1)} %bitcast.3), calls=%async_computation.3 | async-start | bytes 1048576 | tf_op jit(solution)/shard_map/all_to_all | solution.py:285
  61.5 14.5 %structural.2 = bf16[4,8,32,256]{3,2,1,0:T(8,128)(2,1)} custom-call(s32[80]{0:T(128)S(1)} %reshape.30.table_ref, s32[1]{0:T(128)} %constant.23.clone.1.offset_ref, bf16[32,64,256]{2,1,0:T(8,128)(2,1)S(1)} %bitcast.8, bf16[256,256]{1,0:T(8,128)(2,1)S(1)} %copy-done.3, bf16[256,512]{1,0:T(8,128)(2,1)S(1)} %copy-done.1, bf16[256,256]{1,0:T(8,128)(2,1)S(1)} %copy-done.4), custom_call_target="tpu_custom_call" | custom-call | tf_op jit(solution)/shard_map/structural/pallas_call | solution.py:149
  76.0 1.8 %all-to-all-done.3.h_ref = bf16[32,32,256]{2,1,0:T(8,128)(2,1)S(1)} async-done(((bf16[32,32,256]{2,1,0:T(8,128)(2,1)}), bf16[32,32,256]{2,1,0:T(8,128)(2,1)S(1)}, u32[]{:S(2)}, u32[]{:S(2)}) %all-to-all-start.3) | async-done | bytes 524320 | tf_op jit(solution)/shard_map/all_to_all | solution.py:285
  77.7 4.3 %all-to-all-start.2 = ((bf16[32,32,256]{2,1,0:T(8,128)(2,1)}), bf16[32,32,256]{2,1,0:T(8,128)(2,1)S(1)}, u32[]{:S(2)}, u32[]{:S(2)}) async-start(bf16[32,32,256]{2,1,0:T(8,128)(2,1)} %bitcast.2), calls=%async_computation.2 | async-start | bytes 1048576 | tf_op jit(solution)/shard_map/all_to_all | solution.py:285
  82.0 0.1 dynamic_slice.3
  82.1 0.1 fusion
  82.2 0.1 broadcast_in_dim.23
  82.3 0.1 broadcast_in_dim.20
  82.3 0.1 broadcast_in_dim.21
  82.4 0.1 broadcast_in_dim.22.birth_ref
  82.5 0.1 broadcast_in_dim.24
  82.6 0.1 broadcast_in_dim.25.birth_ref
  82.7 0.0 copy-done.5
  82.7 5.6 %temporal.2.refs_0_ = f32[32,64,256]{2,1,0:T(8,128)} custom-call(bf16[32,32,256]{2,1,0:T(8,128)(2,1)S(1)} %all-to-all-done.3.h_ref, s32[8,128]{1,0:T(8,128)S(1)} %broadcast_in_dim.25.birth_ref, bf16[32,256]{1,0:T(8,128)(2,1)S(1)} %copy-done.5, bf16[256,768]{1,0:T(8,128)(2,1)S(1)} %copy-done, bf16[256,256]{1,0:T(8,128)(2,1)S(1)} %copy-done.2), custom_call_target="tpu_custom_call" | custom-call | tf_op jit(solution)/shard_map/temporal/pallas_call | solution.py:234
  88.3 9.8 %all-to-all-done.2.h_ref = bf16[32,32,256]{2,1,0:T(8,128)(2,1)S(1)} async-done(((bf16[32,32,256]{2,1,0:T(8,128)(2,1)}), bf16[32,32,256]{2,1,0:T(8,128)(2,1)S(1)}, u32[]{:S(2)}, u32[]{:S(2)}) %all-to-all-start.2) | async-done | bytes 524320 | tf_op jit(solution)/shard_map/all_to_all | solution.py:285
  98.1 5.6 %temporal.3 = f32[32,64,256]{2,1,0:T(8,128)} custom-call(bf16[32,32,256]{2,1,0:T(8,128)(2,1)S(1)} %all-to-all-done.2.h_ref, s32[8,128]{1,0:T(8,128)S(1)} %broadcast_in_dim.22.birth_ref, bf16[32,256]{1,0:T(8,128)(2,1)S(1)} %copy-done.5, bf16[256,768]{1,0:T(8,128)(2,1)S(1)} %copy-done, bf16[256,256]{1,0:T(8,128)(2,1)S(1)} %copy-done.2, ...), custom_call_target="tpu_custom_call", output_to_operand_aliasing={{}: (5, {})} | custom-call | tf_op jit(solution)/shard_map/temporal/pallas_call | solution.py:234
  (13 shorter events, 0.0 us)
Async XLA Ops:
  0.0 43.5 %copy-start.4 = (bf16[256,256]{1,0:T(8,128)(2,1)S(1)}, bf16[256,256]{1,0:T(8,128)(2,1)}, u32[]{:S(2)}) copy-start(bf16[256,256]{1,0:T(8,128)(2,1)} %wo_ref.5) | copy-start | bytes 393220
  0.0 43.5 %copy-start.1 = (bf16[256,512]{1,0:T(8,128)(2,1)S(1)}, bf16[256,512]{1,0:T(8,128)(2,1)}, u32[]{:S(2)}) copy-start(bf16[256,512]{1,0:T(8,128)(2,1)} %wkv_ref.3) | copy-start | bytes 786436
  0.0 43.5 %copy-start.3 = (bf16[256,256]{1,0:T(8,128)(2,1)S(1)}, bf16[256,256]{1,0:T(8,128)(2,1)}, u32[]{:S(2)}) copy-start(bf16[256,256]{1,0:T(8,128)(2,1)} %wq_ref.3) | copy-start | bytes 393220
  13.4 30.1 %all-to-all-start.1 = ((bf16[8,256,256]{2,1,0:T(8,128)(2,1)}), bf16[8,256,256]{2,1,0:T(8,128)(2,1)S(1)}, u32[]{:S(2)}, u32[]{:S(2)}) async-start(bf16[8,256,256]{2,1,0:T(8,128)(2,1)} %param.10), calls=%async_computation.1 | async-start | bytes 2097152 | tf_op jit(solution)/shard_map/all_to_all | solution.py:273
  58.0 24.0 %copy-start.6 = (s32[256]{0:T(256)S(1)}, s32[256]{0:T(256)}, u32[]{:S(2)}) copy-start(s32[256]{0:T(256)} %param.13) | copy-start | bytes 3076
  58.0 24.7 %copy-start = (bf16[256,768]{1,0:T(8,128)(2,1)S(1)}, bf16[256,768]{1,0:T(8,128)(2,1)}, u32[]{:S(2)}) copy-start(bf16[256,768]{1,0:T(8,128)(2,1)} %wt_ref.3) | copy-start | bytes 1179652
  58.0 24.7 %copy-start.2 = (bf16[256,256]{1,0:T(8,128)(2,1)S(1)}, bf16[256,256]{1,0:T(8,128)(2,1)}, u32[]{:S(2)}) copy-start(bf16[256,256]{1,0:T(8,128)(2,1)} %wo_ref.7) | copy-start | bytes 393220
  58.0 24.7 %copy-start.5 = (bf16[32,256]{1,0:T(8,128)(2,1)S(1)}, bf16[32,256]{1,0:T(8,128)(2,1)}, u32[]{:S(2)}) copy-start(bf16[32,256]{1,0:T(8,128)(2,1)} %pos_ref.3) | copy-start | bytes 49156
  58.0 19.7 %all-to-all-start.3 = ((bf16[32,32,256]{2,1,0:T(8,128)(2,1)}), bf16[32,32,256]{2,1,0:T(8,128)(2,1)S(1)}, u32[]{:S(2)}, u32[]{:S(2)}) async-start(bf16[32,32,256]{2,1,0:T(8,128)(2,1)} %bitcast.3), calls=%async_computation.3 | async-start | bytes 1048576 | tf_op jit(solution)/shard_map/all_to_all | solution.py:285
  77.7 20.3 %all-to-all-start.2 = ((bf16[32,32,256]{2,1,0:T(8,128)(2,1)}), bf16[32,32,256]{2,1,0:T(8,128)(2,1)S(1)}, u32[]{:S(2)}, u32[]{:S(2)}) async-start(bf16[32,32,256]{2,1,0:T(8,128)(2,1)} %bitcast.2), calls=%async_computation.2 | async-start | bytes 1048576 | tf_op jit(solution)/shard_map/all_to_all | solution.py:285

commit v2 on v1

--- a/solution.py
+++ b/solution.py
@@ -269,9 +269,10 @@
     outgoing = features
     if sharers > 1:
         outgoing = jnp.repeat(features, sharers, axis=0)
-        table = jnp.repeat(table, sharers, axis=0)
     snapshot = lax.all_to_all(outgoing, "vert", split_axis=0, concat_axis=0, tiled=True)
-    table = lax.all_to_all(table, "vert", split_axis=0, concat_axis=0, tiled=True).reshape(-1)
+    tables = lax.all_gather(table, "vert", axis=1)
+    own = lax.axis_index("vert") // sharers
+    table = lax.dynamic_index_in_dim(tables, own, 0, keepdims=False).reshape(-1)
     x = snapshot.reshape(peers * groups, quarter, width)
     share = lax.axis_index("vert") % sharers
 

time: 104 us -> 101 us (0.971)
  waiting for transfers between devices: 37.9 us -> 11.6 us
  blocking collectives: 11.8 us -> 32.5 us
  starting transfers between devices: 11.3 us -> 15 us
  local copies, waits for them, and re-layouts: 2.34 us -> 0.94 us
    all_gather x0 -> x1, blocking collectives: none -> 32.5 us  [local(): tables = lax.all_gather(table, 'vert', axis=1)]
    all_to_all x1, waiting for transfers between devices: 26.4 us -> 0.01 us  [local(): lax.all_to_all(outgoing, 'vert', split_axis=0, concat_axis=0, tiled=True)]
    all_to_all x1 -> x0, blocking collectives: 11.8 us -> none  [local(): lax.all_to_all(table, 'vert', split_axis=0, concat_axis=0, tiled=True)]
    all_to_all x1, starting transfers between devices: 3.56 us -> 6.51 us  [local(): lax.all_to_all(outgoing, 'vert', split_axis=0, concat_axis=0, tiled=True)]
  transfers between devices with their start and end apart: 3 -> 3, of which waited for: 3 -> 2; matrix products, arithmetic and copies ran while one was open for 1% -> 1% of each run, Pallas kernels for 19% -> 20%
where the time goes in v2:
time: 101 us; the launch traced here: 100 us
  Pallas kernels  40.1 us (40%)
  blocking collectives  32.5 us (32%)
  starting transfers between devices  15 us (15%)
  waiting for transfers between devices  11.6 us (11%)
    all_gather x1, blocking collectives, local(): tables = lax.all_gather(table, 'vert', axis=1)  32.5 us
    pallas_call x2, Pallas kernels, structural(): pl.pallas_call(functools.partial(structural_kernel, slots=slots), out_sha...  28.9 us
    all_to_all x2, waiting for transfers between devices, local(): lax.all_to_all(hidden, ('snap', 'vert'), split_axis=0, concat_axis=0, til...  11.6 us
    pallas_call x2, Pallas kernels, temporal(): pl.pallas_call(temporal_kernel, grid=(1,), out_shape=jax.ShapeDtypeStruct...  11.2 us
    all_to_all x2, starting transfers between devices, local(): lax.all_to_all(hidden, ('snap', 'vert'), split_axis=0, concat_axis=0, til...  8.45 us
    all_to_all x1, starting transfers between devices, local(): lax.all_to_all(outgoing, 'vert', split_axis=0, concat_axis=0, tiled=True)  6.51 us
  transfers between devices with their start and end apart: 3, of which 2 were waited for; matrix products, arithmetic and copies ran while one was open for 1% of the time, Pallas kernels for 20%

profile of v2, /device:TPU:0, one launch (start us, length us, event | category | flops | bytes accessed | tf_op | source)
XLA Modules:
  0.0 100.3 jit_solution(9272102564193152872)
XLA Ops:
  0.0 6.5 %all-to-all-start = ((bf16[8,256,256]{2,1,0:T(8,128)(2,1)}), bf16[8,256,256]{2,1,0:T(8,128)(2,1)S(1)}, u32[]{:S(2)}, u32[]{:S(2)}) async-start(bf16[8,256,256]{2,1,0:T(8,128)(2,1)} %param.10), calls=%async_computation | async-start | bytes 2097152 | tf_op jit(solution)/shard_map/all_to_all | solution.py:272
  6.5 0.1 copy.18
  6.6 0.1 copy.19
  6.7 0.1 pad_add_fusion
  6.8 32.5 %all-gather = s32[8,16,5]{2,0,1:T(8,128)S(1)} all-gather(s32[8,2,5]{2,0,1:T(8,128)S(1)} %pad_add_fusion), channel_id=2, replica_groups=mesh['snap'=4,'vert'=8] {'vert'}, dimensions={1}, use_global_device_ids=true | all-gather | bytes 2880 | tf_op jit(solution)/shard_map/all_gather | solution.py:273
  39.3 0.1 reshape.31.table_ref
  39.4 0.0 all-to-all-done
  39.4 14.5 %structural.3 = bf16[4,8,32,256]{3,2,1,0:T(8,128)(2,1)} custom-call(s32[80]{0:T(128)S(1)} %reshape.31.table_ref, s32[1]{0:T(128)} %constant.43.clone.1.offset_ref, bf16[32,64,256]{2,1,0:T(8,128)(2,1)S(1)} %bitcast.9, bf16[256,256]{1,0:T(8,128)(2,1)S(1)} %copy-done.3, bf16[256,512]{1,0:T(8,128)(2,1)S(1)} %copy-done.1, bf16[256,256]{1,0:T(8,128)(2,1)S(1)} %copy-done.4), custom_call_target="tpu_custom_call" | custom-call | tf_op jit(solution)/shard_map/structural/pallas_call | solution.py:149
  53.9 4.5 %all-to-all-start.2 = ((bf16[32,32,256]{2,1,0:T(8,128)(2,1)}), bf16[32,32,256]{2,1,0:T(8,128)(2,1)S(1)}, u32[]{:S(2)}, u32[]{:S(2)}) async-start(bf16[32,32,256]{2,1,0:T(8,128)(2,1)} %bitcast.4), calls=%async_computation.2 | async-start | bytes 1048576 | tf_op jit(solution)/shard_map/all_to_all | solution.py:286
  58.4 14.5 %structural.2 = bf16[4,8,32,256]{3,2,1,0:T(8,128)(2,1)} custom-call(s32[80]{0:T(128)S(1)} %reshape.31.table_ref, s32[1]{0:T(128)} %constant.39.clone.1.offset_ref, bf16[32,64,256]{2,1,0:T(8,128)(2,1)S(1)} %bitcast.10, bf16[256,256]{1,0:T(8,128)(2,1)S(1)} %copy-done.3, bf16[256,512]{1,0:T(8,128)(2,1)S(1)} %copy-done.1, bf16[256,256]{1,0:T(8,128)(2,1)S(1)} %copy-done.4), custom_call_target="tpu_custom_call" | custom-call | tf_op jit(solution)/shard_map/structural/pallas_call | solution.py:149
  72.9 1.8 %all-to-all-done.2.h_ref = bf16[32,32,256]{2,1,0:T(8,128)(2,1)S(1)} async-done(((bf16[32,32,256]{2,1,0:T(8,128)(2,1)}), bf16[32,32,256]{2,1,0:T(8,128)(2,1)S(1)}, u32[]{:S(2)}, u32[]{:S(2)}) %all-to-all-start.2) | async-done | bytes 524320 | tf_op jit(solution)/shard_map/all_to_all | solution.py:286
  74.6 4.0 %all-to-all-start.1 = ((bf16[32,32,256]{2,1,0:T(8,128)(2,1)}), bf16[32,32,256]{2,1,0:T(8,128)(2,1)S(1)}, u32[]{:S(2)}, u32[]{:S(2)}) async-start(bf16[32,32,256]{2,1,0:T(8,128)(2,1)} %bitcast.3), calls=%async_computation.1 | async-start | bytes 1048576 | tf_op jit(solution)/shard_map/all_to_all | solution.py:286
  78.6 0.1 dynamic_slice.8
  78.7 0.1 fusion
  78.8 0.1 broadcast_in_dim.23
  78.8 0.1 broadcast_in_dim.20
  78.9 0.1 broadcast_in_dim.21
  79.0 0.1 broadcast_in_dim.22.birth_ref
  79.1 0.1 broadcast_in_dim.24
  79.1 0.1 broadcast_in_dim.25.birth_ref
  79.2 0.0 copy-done.5
  79.3 5.6 %temporal.2.refs_0_ = f32[32,64,256]{2,1,0:T(8,128)} custom-call(bf16[32,32,256]{2,1,0:T(8,128)(2,1)S(1)} %all-to-all-done.2.h_ref, s32[8,128]{1,0:T(8,128)S(1)} %broadcast_in_dim.25.birth_ref, bf16[32,256]{1,0:T(8,128)(2,1)S(1)} %copy-done.5, bf16[256,768]{1,0:T(8,128)(2,1)S(1)} %copy-done, bf16[256,256]{1,0:T(8,128)(2,1)S(1)} %copy-done.2), custom_call_target="tpu_custom_call" | custom-call | tf_op jit(solution)/shard_map/temporal/pallas_call | solution.py:234
  84.9 9.8 %all-to-all-done.1.h_ref = bf16[32,32,256]{2,1,0:T(8,128)(2,1)S(1)} async-done(((bf16[32,32,256]{2,1,0:T(8,128)(2,1)}), bf16[32,32,256]{2,1,0:T(8,128)(2,1)S(1)}, u32[]{:S(2)}, u32[]{:S(2)}) %all-to-all-start.1) | async-done | bytes 524320 | tf_op jit(solution)/shard_map/all_to_all | solution.py:286
  94.6 5.6 %temporal.3 = f32[32,64,256]{2,1,0:T(8,128)} custom-call(bf16[32,32,256]{2,1,0:T(8,128)(2,1)S(1)} %all-to-all-done.1.h_ref, s32[8,128]{1,0:T(8,128)S(1)} %broadcast_in_dim.22.birth_ref, bf16[32,256]{1,0:T(8,128)(2,1)S(1)} %copy-done.5, bf16[256,768]{1,0:T(8,128)(2,1)S(1)} %copy-done, bf16[256,256]{1,0:T(8,128)(2,1)S(1)} %copy-done.2, ...), custom_call_target="tpu_custom_call", output_to_operand_aliasing={{}: (5, {})} | custom-call | tf_op jit(solution)/shard_map/temporal/pallas_call | solution.py:234
  (18 shorter events, 0.0 us)
Async XLA Ops:
  0.0 6.5 %copy-start.6 = (s32[8,2,4]{0,2,1:T(4,128)S(1)}, s32[8,2,4]{0,2,1:T(4,128)}, u32[]{:S(2)}) copy-start(s32[8,2,4]{0,2,1:T(4,128)} %param.11) | copy-start | bytes 772
  0.0 6.6 %copy-start.7 = (s32[8,2]{0,1:T(2,128)S(1)}, s32[8,2]{0,1:T(2,128)}, u32[]{:S(2)}) copy-start(s32[8,2]{0,1:T(2,128)} %param.12) | copy-start | bytes 196
  0.0 39.4 %copy-start.4 = (bf16[256,256]{1,0:T(8,128)(2,1)S(1)}, bf16[256,256]{1,0:T(8,128)(2,1)}, u32[]{:S(2)}) copy-start(bf16[256,256]{1,0:T(8,128)(2,1)} %wo_ref.5) | copy-start | bytes 393220
  0.0 39.4 %copy-start.1 = (bf16[256,512]{1,0:T(8,128)(2,1)S(1)}, bf16[256,512]{1,0:T(8,128)(2,1)}, u32[]{:S(2)}) copy-start(bf16[256,512]{1,0:T(8,128)(2,1)} %wkv_ref.3) | copy-start | bytes 786436
  0.0 39.4 %copy-start.3 = (bf16[256,256]{1,0:T(8,128)(2,1)S(1)}, bf16[256,256]{1,0:T(8,128)(2,1)}, u32[]{:S(2)}) copy-start(bf16[256,256]{1,0:T(8,128)(2,1)} %wq_ref.3) | copy-start | bytes 393220
  0.0 39.4 %all-to-all-start = ((bf16[8,256,256]{2,1,0:T(8,128)(2,1)}), bf16[8,256,256]{2,1,0:T(8,128)(2,1)S(1)}, u32[]{:S(2)}, u32[]{:S(2)}) async-start(bf16[8,256,256]{2,1,0:T(8,128)(2,1)} %param.10), calls=%async_computation | async-start | bytes 2097152 | tf_op jit(solution)/shard_map/all_to_all | solution.py:272
  53.9 24.7 %copy-start.8 = (s32[256]{0:T(256)S(1)}, s32[256]{0:T(256)}, u32[]{:S(2)}) copy-start(s32[256]{0:T(256)} %param.13) | copy-start | bytes 3076
  53.9 25.4 %copy-start = (bf16[256,768]{1,0:T(8,128)(2,1)S(1)}, bf16[256,768]{1,0:T(8,128)(2,1)}, u32[]{:S(2)}) copy-start(bf16[256,768]{1,0:T(8,128)(2,1)} %wt_ref.3) | copy-start | bytes 1179652
  53.9 25.4 %copy-start.2 = (bf16[256,256]{1,0:T(8,128)(2,1)S(1)}, bf16[256,256]{1,0:T(8,128)(2,1)}, u32[]{:S(2)}) copy-start(bf16[256,256]{1,0:T(8,128)(2,1)} %wo_ref.7) | copy-start | bytes 393220
  53.9 25.4 %copy-start.5 = (bf16[32,256]{1,0:T(8,128)(2,1)S(1)}, bf16[32,256]{1,0:T(8,128)(2,1)}, u32[]{:S(2)}) copy-start(bf16[32,256]{1,0:T(8,128)(2,1)} %pos_ref.3) | copy-start | bytes 49156
  53.9 20.7 %all-to-all-start.2 = ((bf16[32,32,256]{2,1,0:T(8,128)(2,1)}), bf16[32,32,256]{2,1,0:T(8,128)(2,1)S(1)}, u32[]{:S(2)}, u32[]{:S(2)}) async-start(bf16[32,32,256]{2,1,0:T(8,128)(2,1)} %bitcast.4), calls=%async_computation.2 | async-start | bytes 1048576 | tf_op jit(solution)/shard_map/all_to_all | solution.py:286
  74.6 20.0 %all-to-all-start.1 = ((bf16[32,32,256]{2,1,0:T(8,128)(2,1)}), bf16[32,32,256]{2,1,0:T(8,128)(2,1)S(1)}, u32[]{:S(2)}, u32[]{:S(2)}) async-start(bf16[32,32,256]{2,1,0:T(8,128)(2,1)} %bitcast.3), calls=%async_computation.1 | async-start | bytes 1048576 | tf_op jit(solution)/shard_map/all_to_all | solution.py:286

commit v3 on v1

--- a/solution.py
+++ b/solution.py
@@ -11,6 +11,7 @@
 HEADS = 8
 TILE = 128
 CHUNKS = 2
+TOGETHER = 16
 F32 = jnp.float32
 BF16 = jnp.bfloat16
 
@@ -46,11 +47,11 @@
 
 
 def structural_kernel(
-    table_ref,
     offset_ref,
     x_ref,
     wq_ref,
-    wkv_ref,
+    wk_ref,
+    wvt_ref,
     wo_ref,
     out_ref,
     k_ref,
@@ -59,109 +60,156 @@
     s_ref,
     p_ref,
     a_ref,
+    loaded_ref,
+    table_ref,
+    table_sem,
     *,
     slots,
 ):
-    pieces, piece_rows, width = x_ref.shape
-    groups, peers, rows, _ = out_ref.shape
+    peers, _, width = x_ref.shape
+    groups, _, rows, _ = out_ref.shape
+    total = k_ref.shape[0]
+    vert_rows = total // peers
+    quarter = vert_rows // groups
     half = width // 2
+    half_heads = HEADS // 2
     head_size = width // HEADS
-    total = pieces * piece_rows
+    blocks = vert_rows // TILE
     row_blocks = total // TILE
-    block_rows = pieces * rows // row_blocks
+    pieces = TILE // quarter
+    span = pieces * rows
+    lanes = half_heads * span
+    units = s_ref.shape[0]
+    merged = min(blocks, 128 // span)
     factor = head_size ** (-0.5) * math.log2(math.e)
-    step = 2 * TILE
-    pieces_per_step = step // piece_rows
+    for i in range(peers):
+        tail = x_ref[i, vert_rows:, :128].astype(F32)
+        loaded_ref[i : i + 1, :] = tail[:1].astype(jnp.int32)
+    load = pltpu.make_async_copy(loaded_ref, table_ref, table_sem)
+    load.start()
 
     def project(i, carry):
-        at = pl.ds(pl.multiple_of(i * step, step), step)
-        x = x_ref[pl.ds(i * pieces_per_step, pieces_per_step)].reshape(step, width)
-        keyval = matmul(x, wkv_ref[...]).astype(BF16)
-        k_ref[at, :] = keyval[:, :width]
-        ones = jnp.ones((step, half), BF16)
-        v_ref[at, :] = jnp.concatenate(
-            [keyval[:, width : width + half], ones, keyval[:, width + half :], ones], axis=1
-        )
+        at = pl.ds(pl.multiple_of(i * vert_rows, vert_rows), vert_rows)
+        x = x_ref[i, :vert_rows, :]
+        k_ref[at, :] = matmul(x, wk_ref[...]).astype(BF16)
+        values = contract_last(wvt_ref[...], x).astype(BF16)
+        v_ref[0, :half, at] = values[:half]
+        v_ref[1, :half, at] = values[half:]
         return carry
 
-    lax.fori_loop(0, total // step, project, 0)
+    lax.fori_loop(0, peers, project, 0, unroll=2)
+    v_ref[:, half:, :total] = jnp.ones((2, v_ref.shape[1] - half, total), BF16)
+    v_ref[:, :, total:] = jnp.zeros((2, v_ref.shape[1], TILE), BF16)
     offset = pl.multiple_of(offset_ref[0], rows)
-    x_rows = x_ref[:, pl.ds(offset, rows), :].reshape(pieces * rows, width)
-    q_ref[...] = matmul(x_rows, wq_ref[...]).astype(BF16)
-
-    def attend(r, tiles):
-        count = table_ref[r * (slots + 1) + slots]
-        at = pl.ds(pl.multiple_of(r * block_rows, block_rows), block_rows)
-        spots = []
-        for t in range(tiles):
-            spot = jnp.maximum(table_ref[r * (slots + 1) + t], 0)
-            spots.append(pl.ds(pl.multiple_of(spot * TILE, TILE), TILE))
-        queries = spread_heads(q_ref[at, :], head_size)
-        keys = jnp.concatenate([k_ref[spot, :] for spot in spots], axis=0)
-        s_ref[:, : tiles * TILE] = contract_last(queries, keys)
-        for h in range(HEADS):
-            part = slice(h * block_rows, (h + 1) * block_rows)
-            scores = []
-            for t in range(tiles):
-                score = s_ref[part, t * TILE : (t + 1) * TILE]
-                if t == tiles - 1 and t > 0:
-                    score = score + jnp.where(count > t, 0.0, -jnp.inf)
-                scores.append(score)
-            top = scores[0]
-            for score in scores[1:]:
-                top = jnp.maximum(top, score)
-            top = jnp.max(top, axis=1, keepdims=True)
-            for t in range(tiles):
-                p_ref[part, t * TILE : (t + 1) * TILE] = jnp.exp2(
-                    (scores[t] - top) * factor
+    for g in range(groups):
+        x_rows = x_ref[:, pl.ds(offset + g * quarter, rows), :].reshape(peers * rows, width)
+        q_ref[g] = (
+            (matmul(x_rows, wq_ref[...]) * factor).astype(BF16).reshape(peers, rows, width)
+        )
+
+    load.wait()
+
+    def read_slots(peer, block):
+        base = block * (slots + 1)
+        count = table_ref[peer, base + slots]
+        first = table_ref[peer, base]
+        keys = []
+        values = []
+        for t in range(slots):
+            spot = table_ref[peer, base + t]
+            key = jnp.where(count > t, spot, first)
+            value = jnp.where(count > t, spot, row_blocks)
+            keys.append(pl.ds(pl.multiple_of(key * TILE, TILE), TILE))
+            values.append(pl.ds(pl.multiple_of(value * TILE, TILE), TILE))
+        return keys, values
+
+    def score(unit, peer, block):
+        keys, _ = read_slots(peer, block)
+        queries = jnp.concatenate(
+            [q_ref[block * pieces + i, peer] for i in range(pieces)], axis=0
+        )
+        keys = jnp.concatenate([k_ref[key, :] for key in keys], axis=0)
+        s_ref[unit] = contract_last(keys, spread_heads(queries, head_size))
+
+    def blend(unit, peer, block):
+        _, values = read_slots(peer, block)
+        parts = []
+        for j in range(2):
+            for c in range(j * lanes, (j + 1) * lanes, 128):
+                top = jnp.max(s_ref[unit, :, c : c + 128], axis=0, keepdims=True)
+                p_ref[unit, :, c : c + 128] = jnp.exp2(
+                    s_ref[unit, :, c : c + 128] - top
                 ).astype(BF16)
-        values = jnp.concatenate([v_ref[spot, :] for spot in spots], axis=0)
-        middle = HEADS // 2 * block_rows
-        low = matmul(p_ref[:middle, : tiles * TILE], values[:, :width])
-        high = matmul(p_ref[middle:, : tiles * TILE], values[:, width:])
-        a_ref[at, :] = gather_heads(low, high, block_rows, head_size).astype(BF16)
-
-    def row_block(r, carry):
-        count = table_ref[r * (slots + 1) + slots]
-        for tiles in range(2, slots + 1, 2):
-            least = tiles - 2
-
-            @pl.when((count > least) & (count <= tiles))
-            def _(tiles=tiles):
-                attend(r, tiles)
-
+            value = jnp.concatenate([v_ref[j, :, spot] for spot in values], axis=1)
+            mixed = matmul(value, p_ref[unit, :, j * lanes : (j + 1) * lanes])
+            for h in range(half_heads):
+                c = h * span // 128 * 128
+                part = mixed[h * head_size : (h + 1) * head_size, c : c + 128]
+                part = part / mixed[half : half + 1, c : c + 128]
+                shift = (block % merged - h) * span % 128
+                if shift:
+                    part = pltpu.roll(part, shift, 1)
+                parts.append(part)
+        return jnp.concatenate(parts, axis=0)
+
+    def some_peers(i, carry):
+        todo = [(p, b) for p in range(units // blocks) for b in range(blocks)]
+        lane = lax.broadcasted_iota(jnp.int32, (1, 128), 1) // span
+        score(0, i * (units // blocks), 0)
+        wide = None
+        for n, (p, b) in enumerate(todo):
+            if n + 1 < len(todo):
+                score(n + 1, i * (units // blocks) + todo[n + 1][0], todo[n + 1][1])
+            peer = i * (units // blocks) + p
+            part = blend(n, peer, b)
+            wide = part if b % merged == 0 else jnp.where(lane == b % merged, part, wide)
+            if b % merged == merged - 1:
+                narrow = wide.T[: merged * span].astype(BF16)
+                for n in range(merged * pieces):
+                    g = (b + 1 - merged) * pieces + n
+                    a_ref[g, peer] = narrow[n * rows : (n + 1) * rows]
         return carry
 
-    lax.fori_loop(0, row_blocks, row_block, 0)
-    update = matmul(a_ref[...], wo_ref[...])
-    hidden = (x_rows.astype(F32) + update).astype(BF16).reshape(peers, groups, rows, width)
+    lax.fori_loop(0, row_blocks // units, some_peers, 0)
     for g in range(groups):
-        out_ref[g] = hidden[:, g]
-
-
-def structural(table, offset, x, query_proj, keyval_proj, struct_out, rows, groups, slots):
-    pieces, piece_rows, width = x.shape
-    peers = pieces // groups
-    total = pieces * piece_rows
-    block_rows = TILE // piece_rows * rows
+        update = matmul(a_ref[g].reshape(peers * rows, width), wo_ref[...])
+        x_rows = x_ref[:, pl.ds(offset + g * quarter, rows), :].reshape(peers * rows, width)
+        hidden = (x_rows.astype(F32) + update).astype(BF16)
+        out_ref[g] = hidden.reshape(peers, rows, width)
+
+
+def structural(offset, x, query_proj, keyval_proj, struct_out, vert_rows, rows, groups, slots):
+    peers, _, width = x.shape
+    total = peers * vert_rows
+    span = TILE // (vert_rows // groups) * rows
     vmem = pl.BlockSpec(memory_space=pltpu.VMEM)
     smem = pl.BlockSpec(memory_space=pltpu.SMEM)
     return pl.pallas_call(
         functools.partial(structural_kernel, slots=slots),
         out_shape=jax.ShapeDtypeStruct((groups, peers, rows, width), BF16),
-        in_specs=[smem, smem, vmem, vmem, vmem, vmem],
+        in_specs=[smem, vmem, vmem, vmem, vmem, vmem],
         out_specs=vmem,
         scratch_shapes=[
             pltpu.VMEM((total, width), BF16),
-            pltpu.VMEM((total, 2 * width), BF16),
-            pltpu.VMEM((pieces * rows, width), BF16),
-            pltpu.VMEM((HEADS * block_rows, slots * TILE), F32),
-            pltpu.VMEM((HEADS * block_rows, slots * TILE), BF16),
-            pltpu.VMEM((pieces * rows, width), BF16),
+            pltpu.VMEM((2, width // 2 + 16, total + TILE), BF16),
+            pltpu.VMEM((groups, peers, rows, width), BF16),
+            pltpu.VMEM((TOGETHER, slots * TILE, HEADS * span), F32),
+            pltpu.VMEM((TOGETHER, slots * TILE, HEADS * span), BF16),
+            pltpu.VMEM((groups, peers, rows, width), BF16),
+            pltpu.VMEM((peers, 128), jnp.int32),
+            pltpu.SMEM((peers, 128), jnp.int32),
+            pltpu.SemaphoreType.DMA,
         ],
         compiler_params=pltpu.CompilerParams(vmem_limit_bytes=48 * 1024 * 1024),
         name="structural",
-    )(table, offset, x, query_proj, keyval_proj, struct_out)
+    )(
+        offset,
+        x,
+        query_proj,
+        keyval_proj[:, :width],
+        keyval_proj[:, width:].T,
+        struct_out,
+    )
 
 
 def temporal_kernel(h_ref, birth_ref, pos_ref, wt_ref, wo_ref, *refs):
@@ -265,21 +313,20 @@
     chunks = max(1, min(CHUNKS, quarter // (sharers * 16)))
     rows = quarter // (sharers * chunks)
 
-    table = jnp.concatenate([tile_cols, counts[:, :, None]], axis=2)
-    outgoing = features
+    table = jnp.concatenate([tile_cols, counts[:, :, None]], axis=2).astype(BF16)
+    table = table.reshape(snap_count, 1, -1)
+    table = jnp.pad(table, ((0, 0), (0, 15), (0, width - table.shape[2])))
+    outgoing = jnp.concatenate([features, table], axis=1)
     if sharers > 1:
-        outgoing = jnp.repeat(features, sharers, axis=0)
-        table = jnp.repeat(table, sharers, axis=0)
-    snapshot = lax.all_to_all(outgoing, "vert", split_axis=0, concat_axis=0, tiled=True)
-    table = lax.all_to_all(table, "vert", split_axis=0, concat_axis=0, tiled=True).reshape(-1)
-    x = snapshot.reshape(peers * groups, quarter, width)
+        outgoing = jnp.repeat(outgoing, sharers, axis=0)
+    x = lax.all_to_all(outgoing, "vert", split_axis=0, concat_axis=0, tiled=True)
     share = lax.axis_index("vert") % sharers
 
     arrived = []
     for c in range(chunks):
         offset = jnp.reshape((c * sharers + share) * rows, (1,)).astype(jnp.int32)
         hidden = structural(
-            table, offset, x, query_proj, keyval_proj, struct_out, rows, groups, slots
+            offset, x, query_proj, keyval_proj, struct_out, vert_rows, rows, groups, slots
         )
         hidden = hidden.reshape(groups * peers, rows, width)
         hidden = lax.all_to_all(

time: 104 us -> 91.6 us (0.88)
  blocking collectives: 11.8 us -> 0 us
  Pallas kernels: 40.2 us -> 28.6 us
  waiting for transfers between devices: 37.9 us -> 44.9 us
  other arithmetic: 0.08 us -> 3.73 us
  starting transfers between devices: 11.3 us -> 12.9 us
  local copies, waits for them, and re-layouts: 2.34 us -> 0.91 us
    all_to_all x1 -> x0, blocking collectives: 11.8 us -> none  [local(): lax.all_to_all(table, 'vert', split_axis=0, concat_axis=0, tiled=True)]
    pallas_call x2, Pallas kernels: 29 us -> 17.4 us  [structural(): pl.pallas_call(functools.partial(structural_kernel, slots=slots), out_sha...]
    all_to_all x2, waiting for transfers between devices: 11.5 us -> 17.1 us  [local(): lax.all_to_all(hidden, ('snap', 'vert'), split_axis=0, concat_axis=0, til...]
    all_to_all x1, starting transfers between devices: 3.56 us -> 6.35 us  [local(): lax.all_to_all(outgoing, 'vert', split_axis=0, concat_axis=0, tiled=True)]
    concatenate x1 -> x2, other arithmetic: 0.08 us -> 2.36 us  [the longest x1 2.35 us: local(): outgoing = jnp.concatenate([features, table], axis=1)]
    all_to_all x1, waiting for transfers between devices: 26.4 us -> 27.8 us  [local(): lax.all_to_all(outgoing, 'vert', split_axis=0, concat_axis=0, tiled=True)]
    all_to_all x2, starting transfers between devices: 7.78 us -> 6.54 us  [local(): lax.all_to_all(hidden, ('snap', 'vert'), split_axis=0, concat_axis=0, til...]
  transfers between devices with their start and end apart: 3 -> 3, of which waited for: 3 -> 3; matrix products, arithmetic and copies ran while one was open for 1% -> 1% of each run, Pallas kernels for 19% -> 16%
where the time goes in v3:
time: 91.6 us; the launch traced here: 91.1 us
  waiting for transfers between devices  44.9 us (49%)
  Pallas kernels  28.6 us (31%)
  starting transfers between devices  12.9 us (14%)
  other arithmetic  3.73 us (4%)
    all_to_all x1, waiting for transfers between devices, local(): lax.all_to_all(outgoing, 'vert', split_axis=0, concat_axis=0, tiled=True)  27.8 us
    pallas_call x2, Pallas kernels, structural(): pl.pallas_call(functools.partial(structural_kernel, slots=slots), out_sha...  17.4 us
    all_to_all x2, waiting for transfers between devices, local(): lax.all_to_all(hidden, ('snap', 'vert'), split_axis=0, concat_axis=0, til...  17.1 us
    pallas_call x2, Pallas kernels, temporal(): pl.pallas_call(temporal_kernel, grid=(1,), out_shape=jax.ShapeDtypeStruct...  11.2 us
    all_to_all x2, starting transfers between devices, local(): lax.all_to_all(hidden, ('snap', 'vert'), split_axis=0, concat_axis=0, til...  6.54 us
    all_to_all x1, starting transfers between devices, local(): lax.all_to_all(outgoing, 'vert', split_axis=0, concat_axis=0, tiled=True)  6.35 us
    concatenate x1, other arithmetic, local(): outgoing = jnp.concatenate([features, table], axis=1)  2.35 us
  transfers between devices with their start and end apart: 3, of which 3 were waited for; matrix products, arithmetic and copies ran while one was open for 1% of the time, Pallas kernels for 16%

profile of v3, /device:TPU:0, one launch (start us, length us, event | category | flops | bytes accessed | tf_op | source)
XLA Modules:
  0.0 91.1 jit_solution(8606153832229902092)
XLA Ops:
  0.0 0.7 convert_bitcast_fusion
  0.7 0.7 convert.7
  1.4 0.1 copy.19
  1.5 2.3 %fusion.1 = bf16[8,272,256]{2,1,0:T(8,128)(2,1)} fusion(bf16[8,1,10]{2,1,0:T(2,128)(2,1)S(1)} %copy.19, bf16[8,256,256]{2,1,0:T(8,128)(2,1)} %param.10), kind=kLoop, calls=%fused_computation.2 | loop fusion | flops 3342336 | bytes 2162848 | tf_op jit(solution)/shard_map/concatenate | solution.py:319
  3.9 6.4 %all-to-all-start = ((bf16[8,272,256]{2,1,0:T(8,128)(2,1)}), bf16[8,272,256]{2,1,0:T(8,128)(2,1)S(1)}, u32[]{:S(2)}, u32[]{:S(2)}) async-start(bf16[8,272,256]{2,1,0:T(8,128)(2,1)} %fusion.1), calls=%async_computation | async-start | bytes 2228224 | tf_op jit(solution)/shard_map/all_to_all | solution.py:322
  10.3 0.1 copy.24
  10.4 27.8 %all-to-all-done.x_ref = bf16[8,272,256]{2,1,0:T(8,128)(2,1)S(1)} async-done(((bf16[8,272,256]{2,1,0:T(8,128)(2,1)}), bf16[8,272,256]{2,1,0:T(8,128)(2,1)S(1)}, u32[]{:S(2)}, u32[]{:S(2)}) %all-to-all-start) | async-done | bytes 1114144 | tf_op jit(solution)/shard_map/all_to_all | solution.py:322
  38.2 8.7 %structural.3 = bf16[4,8,32,256]{3,2,1,0:T(8,128)(2,1)} custom-call(s32[1]{0:T(128)} %constant.30.clone.1.offset_ref, bf16[8,272,256]{2,1,0:T(8,128)(2,1)S(1)} %all-to-all-done.x_ref, bf16[256,256]{1,0:T(8,128)(2,1)S(1)} %copy-done.1, bf16[256,256]{1,0:T(8,128)(2,1)S(1)} %get-tuple-element.6.wk_ref, bf16[256,256]{1,0:T(8,128)(2,1)S(1)} %bitcast.10, ...), custom_call_target="tpu_custom_call" | custom-call | tf_op jit(solution)/shard_map/structural/pallas_call | solution.py:187
  46.9 3.7 %all-to-all-start.2 = ((bf16[32,32,256]{2,1,0:T(8,128)(2,1)}), bf16[32,32,256]{2,1,0:T(8,128)(2,1)S(1)}, u32[]{:S(2)}, u32[]{:S(2)}) async-start(bf16[32,32,256]{2,1,0:T(8,128)(2,1)} %bitcast.3), calls=%async_computation.2 | async-start | bytes 1048576 | tf_op jit(solution)/shard_map/all_to_all | solution.py:332
  50.6 8.7 %structural.2 = bf16[4,8,32,256]{3,2,1,0:T(8,128)(2,1)} custom-call(s32[1]{0:T(128)} %constant.24.clone.1.offset_ref, bf16[8,272,256]{2,1,0:T(8,128)(2,1)S(1)} %all-to-all-done.x_ref, bf16[256,256]{1,0:T(8,128)(2,1)S(1)} %copy-done.1, bf16[256,256]{1,0:T(8,128)(2,1)S(1)} %get-tuple-element.6.wk_ref, bf16[256,256]{1,0:T(8,128)(2,1)S(1)} %bitcast.11, ...), custom_call_target="tpu_custom_call" | custom-call | tf_op jit(solution)/shard_map/structural/pallas_call | solution.py:187
  59.3 7.4 %all-to-all-done.2.h_ref = bf16[32,32,256]{2,1,0:T(8,128)(2,1)S(1)} async-done(((bf16[32,32,256]{2,1,0:T(8,128)(2,1)}), bf16[32,32,256]{2,1,0:T(8,128)(2,1)S(1)}, u32[]{:S(2)}, u32[]{:S(2)}) %all-to-all-start.2) | async-done | bytes 524320 | tf_op jit(solution)/shard_map/all_to_all | solution.py:332
  66.7 2.8 %all-to-all-start.1 = ((bf16[32,32,256]{2,1,0:T(8,128)(2,1)}), bf16[32,32,256]{2,1,0:T(8,128)(2,1)S(1)}, u32[]{:S(2)}, u32[]{:S(2)}) async-start(bf16[32,32,256]{2,1,0:T(8,128)(2,1)} %bitcast.2), calls=%async_computation.1 | async-start | bytes 1048576 | tf_op jit(solution)/shard_map/all_to_all | solution.py:332
  69.5 0.1 dynamic_slice.3
  69.6 0.1 fusion.3
  69.7 0.1 broadcast_in_dim.24
  69.8 0.1 broadcast_in_dim.21
  69.9 0.1 broadcast_in_dim.22
  69.9 0.1 broadcast_in_dim.23.birth_ref
  70.0 0.1 broadcast_in_dim.25
  70.1 0.1 broadcast_in_dim.26.birth_ref
  70.2 0.0 copy-done.4
  70.2 5.6 %temporal.2.refs_0_ = f32[32,64,256]{2,1,0:T(8,128)} custom-call(bf16[32,32,256]{2,1,0:T(8,128)(2,1)S(1)} %all-to-all-done.2.h_ref, s32[8,128]{1,0:T(8,128)S(1)} %broadcast_in_dim.26.birth_ref, bf16[32,256]{1,0:T(8,128)(2,1)S(1)} %copy-done.4, bf16[256,768]{1,0:T(8,128)(2,1)S(1)} %copy-done, bf16[256,256]{1,0:T(8,128)(2,1)S(1)} %copy-done.3), custom_call_target="tpu_custom_call" | custom-call | tf_op jit(solution)/shard_map/temporal/pallas_call | solution.py:282
  75.8 9.7 %all-to-all-done.1.h_ref = bf16[32,32,256]{2,1,0:T(8,128)(2,1)S(1)} async-done(((bf16[32,32,256]{2,1,0:T(8,128)(2,1)}), bf16[32,32,256]{2,1,0:T(8,128)(2,1)S(1)}, u32[]{:S(2)}, u32[]{:S(2)}) %all-to-all-start.1) | async-done | bytes 524320 | tf_op jit(solution)/shard_map/all_to_all | solution.py:332
  85.5 5.6 %temporal.3 = f32[32,64,256]{2,1,0:T(8,128)} custom-call(bf16[32,32,256]{2,1,0:T(8,128)(2,1)S(1)} %all-to-all-done.1.h_ref, s32[8,128]{1,0:T(8,128)S(1)} %broadcast_in_dim.23.birth_ref, bf16[32,256]{1,0:T(8,128)(2,1)S(1)} %copy-done.4, bf16[256,768]{1,0:T(8,128)(2,1)S(1)} %copy-done, bf16[256,256]{1,0:T(8,128)(2,1)S(1)} %copy-done.3, ...), custom_call_target="tpu_custom_call", output_to_operand_aliasing={{}: (5, {})} | custom-call | tf_op jit(solution)/shard_map/temporal/pallas_call | solution.py:282
  (17 shorter events, 0.1 us)
Async XLA Ops:
  1.5 8.7 %copy-start.5 = (bf16[256,512]{1,0:T(8,128)(2,1)S(1)}, bf16[256,512]{1,0:T(8,128)(2,1)}, u32[]{:S(2)}) copy-start(bf16[256,512]{1,0:T(8,128)(2,1)} %param.15) | copy-start | bytes 786436
  1.5 36.7 %copy-start.1 = (bf16[256,256]{1,0:T(8,128)(2,1)S(1)}, bf16[256,256]{1,0:T(8,128)(2,1)}, u32[]{:S(2)}) copy-start(bf16[256,256]{1,0:T(8,128)(2,1)} %wq_ref.3) | copy-start | bytes 393220
  1.5 36.7 %copy-start.2 = (bf16[256,256]{1,0:T(8,128)(2,1)S(1)}, bf16[256,256]{1,0:T(8,128)(2,1)}, u32[]{:S(2)}) copy-start(bf16[256,256]{1,0:T(8,128)(2,1)} %wo_ref.5) | copy-start | bytes 393220
  3.9 34.3 %all-to-all-start = ((bf16[8,272,256]{2,1,0:T(8,128)(2,1)}), bf16[8,272,256]{2,1,0:T(8,128)(2,1)S(1)}, u32[]{:S(2)}, u32[]{:S(2)}) async-start(bf16[8,272,256]{2,1,0:T(8,128)(2,1)} %fusion.1), calls=%async_computation | async-start | bytes 2228224 | tf_op jit(solution)/shard_map/all_to_all | solution.py:322
  46.9 22.7 %copy-start.6 = (s32[256]{0:T(256)S(1)}, s32[256]{0:T(256)}, u32[]{:S(2)}) copy-start(s32[256]{0:T(256)} %param.13) | copy-start | bytes 3076
  46.9 23.3 %copy-start = (bf16[256,768]{1,0:T(8,128)(2,1)S(1)}, bf16[256,768]{1,0:T(8,128)(2,1)}, u32[]{:S(2)}) copy-start(bf16[256,768]{1,0:T(8,128)(2,1)} %wt_ref.3) | copy-start | bytes 1179652
  46.9 23.3 %copy-start.3 = (bf16[256,256]{1,0:T(8,128)(2,1)S(1)}, bf16[256,256]{1,0:T(8,128)(2,1)}, u32[]{:S(2)}) copy-start(bf16[256,256]{1,0:T(8,128)(2,1)} %wo_ref.7) | copy-start | bytes 393220
  46.9 23.3 %copy-start.4 = (bf16[32,256]{1,0:T(8,128)(2,1)S(1)}, bf16[32,256]{1,0:T(8,128)(2,1)}, u32[]{:S(2)}) copy-start(bf16[32,256]{1,0:T(8,128)(2,1)} %pos_ref.3) | copy-start | bytes 49156
  46.9 19.8 %all-to-all-start.2 = ((bf16[32,32,256]{2,1,0:T(8,128)(2,1)}), bf16[32,32,256]{2,1,0:T(8,128)(2,1)S(1)}, u32[]{:S(2)}, u32[]{:S(2)}) async-start(bf16[32,32,256]{2,1,0:T(8,128)(2,1)} %bitcast.3), calls=%async_computation.2 | async-start | bytes 1048576 | tf_op jit(solution)/shard_map/all_to_all | solution.py:332
  66.7 18.8 %all-to-all-start.1 = ((bf16[32,32,256]{2,1,0:T(8,128)(2,1)}), bf16[32,32,256]{2,1,0:T(8,128)(2,1)S(1)}, u32[]{:S(2)}, u32[]{:S(2)}) async-start(bf16[32,32,256]{2,1,0:T(8,128)(2,1)} %bitcast.2), calls=%async_computation.1 | async-start | bytes 1048576 | tf_op jit(solution)/shard_map/all_to_all | solution.py:332
